TPU v7x, 32 devices: a whole 2x2x4 slice. The times are simulated.
32 devices in a mesh: dp: 4 (over x, y), tp: 8 (over z, core).
Axes of the slice: x: 2, y: 2, z: 4, core: 2. Of those that a mesh axis runs over, the one named last changes fastest.
Arguments:
- x: bfloat16 [8192, 4096], P('dp'), parts along dimension 0
- w_gate: bfloat16 [4096, 10240], P(None, 'tp')
- w_up: bfloat16 [4096, 10240], P(None, 'tp')
- w_down: bfloat16 [10240, 4096], P('tp')
Outputs:
- output: bfloat16 [8192, 4096], P('dp'), parts along dimension 0
There are 4 independent parts. A program takes and returns all parts, laid end to end along the dimension named above; an argument that names none is the same for every part.
All inputs are finite; a program needn't handle non-finite values.
Results may differ from a plain program's by a relative error of at most 0.016.
Values are sent between devices in bfloat16 or wider.
A program may use at most 2 GiB of HBM per device.

v0:
```python
import jax
import jax.numpy as jnp
from jax import lax
from jax.sharding import PartitionSpec as P


def solution(mesh):
    def step(x, w_gate, w_up, w_down):
        gate = jnp.dot(x, w_gate, preferred_element_type=jnp.float32)
        up = jnp.dot(x, w_up, preferred_element_type=jnp.float32)
        hidden = (jax.nn.gelu(gate) * up).astype(jnp.bfloat16)
        term = jnp.dot(hidden, w_down, preferred_element_type=jnp.float32).astype(jnp.bfloat16)
        return lax.psum(term, "tp")

    return jax.shard_map(
        step,
        mesh=mesh,
        in_specs=(P("dp", None), P(None, "tp"), P(None, "tp"), P("tp", None)),
        out_specs=P("dp", None),
        check_vma=False,
    )
```

profile of v0, /device:TPU:0, one launch (start us, length us, event | category | flops | bytes accessed | tf_op | source)
XLA Modules:
  0.0 448.9 jit_solution(18129257449626901574)
XLA Ops:
  6.5 0.0 all-reduce.2.cloned.1.call-start
  6.5 0.0 copy-start
  6.5 29.2 %fusion.13 = f32[2048,1280]{1,0:T(8,128)} fusion(bf16[2048,4096]{1,0:T(8,128)(2,1)} %param.4, bf16[4096,1280]{1,0:T(8,128)(2,1)} %param.5), kind=kOutput, calls=%fused_computation.15 | convolution fusion | flops 21474836480 | bytes 37748736 | tf_op jit(solution)/shard_map/dot_general | solution.py:9
  35.7 0.0 copy-done
  35.7 29.5 %fusion.8.clone.4 = bf16[2048,1280]{1,0:T(8,128)(2,1)S(1)} fusion(f32[2048,1280]{1,0:T(8,128)} %fusion.13, bf16[2048,4096]{1,0:T(8,128)(2,1)S(1)} %copy-done, bf16[4096,1280]{1,0:T(8,128)(2,1)} %param.6), kind=kOutput, calls=%fused_computation.10.clone.clone.clone.1 | convolution fusion | flops 21501050880 | bytes 42991616 | tf_op jit(solution)/shard_map/dot_general | solution.py:10
  65.3 27.2 %convolution_convert_fusion = bf16[2048,4096]{1,0:T(8,128)(2,1)} fusion(bf16[1280,4096]{1,0:T(8,128)(2,1)} %param.7, bf16[2048,1280]{1,0:T(8,128)(2,1)S(1)} %fusion.8.clone.4), kind=kOutput, calls=%fused_computation.1 | convolution fusion | flops 21483225088 | bytes 32505856 | tf_op jit(solution)/shard_map/dot_general | solution.py:12
  92.5 0.0 all-reduce.2.cloned.1.call-update
  92.5 335.5 %all-reduce.2.cloned.1.call-done = bf16[2048,4096]{1,0:T(8,128)(2,1)} async-done(((bf16[2048,4096]{1,0:T(8,128)(2,1)}), bf16[2048,4096]{1,0:T(8,128)(2,1)}) %all-reduce.2.cloned.1.call-update) | async-done | bytes 16777232 | tf_op jit(solution)/shard_map/psum | solution.py:13
  428.0 14.1 %copy.6 = bf16[2048,4096]{1,0:T(8,128)(2,1)} copy(bf16[2048,4096]{1,0:T(8,128)(2,1)} %all-reduce.2.cloned.1.call-done) | data formatting | bytes 33554432
Async XLA Ops:
  6.5 421.5 %all-reduce.2.cloned.1.call-start = ((), (), s32[]{:S(2)}) async-start(), calls=%async_computation | async-start | bytes 33554432 | tf_op jit(solution)/shard_map/psum | solution.py:13
  6.5 29.2 %copy-start = (bf16[2048,4096]{1,0:T(8,128)(2,1)S(1)}, bf16[2048,4096]{1,0:T(8,128)(2,1)}, u32[]{:S(2)}) copy-start(bf16[2048,4096]{1,0:T(8,128)(2,1)} %param.4) | copy-start | bytes 50331652
Sparse Core Ops, SparseCore 0:
  92.6 335.3 all-reduce.1
where the time goes:
time: 449 us
  waiting for transfers between devices  336 us (75%)
  matrix products  85.9 us (19%)
  local copies, waits for them, and re-layouts  14.1 us (3%)
  between operations  13.4 us (3%)
    psum x1, waiting for transfers between devices, step(): return lax.psum(term, 'tp')  336 us
    dot_general x1, matrix products, step(): up = jnp.dot(x, w_up, preferred_element_type=jnp.float32)  29.5 us
    dot_general x1, matrix products, step(): gate = jnp.dot(x, w_gate, preferred_element_type=jnp.float32)  29.2 us
    dot_general x1, matrix products, step(): jnp.dot(hidden, w_down, preferred_element_type=jnp.float32)  27.2 us
    unnamed x3, local copies, waits for them, and re-layouts  14.1 us
  transfers between devices with their start and end apart: 1, of which 1 were waited for; matrix products, arithmetic and copies ran while one was open for 0% of the time, Pallas kernels for 0%

commit v1 on v0

v1 whole, which is shorter than its diff:
```python
import functools

import jax
import jax.numpy as jnp
from jax import lax
from jax.experimental import pallas as pl
from jax.experimental.pallas import tpu as pltpu
from jax.sharding import PartitionSpec as P

MESH = pl.DeviceIdType.MESH

LANE = 128
PW = 512
HB = 256
RS = 12
RO = 12
SS = 4
LS = 8
LA, LO, LF, LE = 0, 2, 4, 8


def _kernel(cfg, x, wg, wu, wd, y, wgv, wuv, wdv, xb, hid, own, sibr, innr, sst, lst,
            wg_m, wu_m, wd_m, x_m, sib_s, sib_r, lk_s, out_r, inn_r, fin_r, sf_r,
            fs_sib, fs_out, fs_inn, credit):
    rows, d, ff, lane, pw, hb = cfg
    nc, npc, nh = rows // (2 * lane), d // pw, ff // hb
    nq = nc * npc
    me = lax.axis_index("tp")
    z, c = me // 2, me % 2
    end = (z * (3 - z)) == 0
    mid = (z * (3 - z)) != 0
    sib = {"tp": 2 * z + 1 - c}
    inner = {"tp": 2 * (1 + z % 2) + c}
    outer = {"tp": 6 * (z // 2) + c}

    def x_copies(s, slot):
        return [
            pltpu.make_async_copy(
                x.at[pl.ds(pl.multiple_of((2 * s + lax.rem(c + h, 2)) * lane, lane), lane)],
                xb.at[slot, pl.ds(h * lane, lane)], x_m.at[slot, h])
            for h in range(2)
        ]

    def w_copy(src, dst, sem, j, width):
        cols = pl.ds(pl.multiple_of(j * width, width), width)
        return pltpu.make_async_copy(src.at[:, cols], dst.at[:, cols], sem.at[j])

    for cp in x_copies(0, 0):
        cp.start()
    for j in range(nh):
        w_copy(wg, wgv, wg_m, j, hb).start()
        w_copy(wu, wuv, wu_m, j, hb).start()
    for j in range(npc):
        w_copy(wd, wdv, wd_m, j, pw).start()
    for cp in x_copies(1, 1):
        cp.start()

    bar = pltpu.get_barrier_semaphore()
    pl.semaphore_signal(bar, inc=1, device_id=sib, device_id_type=MESH)
    pl.semaphore_signal(bar, inc=1, device_id=inner, device_id_type=MESH)

    @pl.when(mid)
    def _():
        pl.semaphore_signal(bar, inc=1, device_id=outer, device_id_type=MESH)
        pl.semaphore_wait(bar, 3)

    @pl.when(end)
    def _():
        pl.semaphore_wait(bar, 2)

    def at(q, ln):
        s, i = q // npc, q % npc
        return (pl.ds(pl.multiple_of((2 * s + ln) * lane, lane), lane),
                pl.ds(pl.multiple_of(i * pw, pw), pw))

    def remote(src, dst, ss, rs, to):
        return pltpu.make_async_remote_copy(
            src_ref=src, dst_ref=dst, send_sem=ss, recv_sem=rs, device_id=to, device_id_type=MESH)

    def sib_copy(q):
        return remote(sst.at[q % SS], sibr.at[q % RS], sib_s.at[q % SS], sib_r.at[q % RS], sib)

    def end_copy(q):
        r = at(q, c)
        return remote(lst.at[q % LS], y.at[r], lk_s.at[q % LS], out_r.at[q], inner)

    def inn_copy(q):
        k = q // 2
        return remote(lst.at[k % LS], innr.at[k], lk_s.at[k % LS], inn_r.at[k], inner)

    def fin_sib(q):
        r = at(q, c)
        return remote(y.at[r], y.at[r], fs_sib.at[q], sf_r.at[q], sib)

    def fin_out(q):
        r = at(q, c)
        return remote(y.at[r], y.at[r], fs_out.at[q], fin_r.at[q], outer)

    def fin_inn(q):
        r = at(q, c)
        return remote(y.at[r], y.at[r], fs_inn.at[q // 2], fin_r.at[q], inner)

    def sib_fin_in(q):
        r = at(q, 1 - c)
        return remote(y.at[r], y.at[r], fs_sib.at[q], sf_r.at[q], sib)

    def gate_up(s, j):
        slot = s % 2

        @pl.when(j == 0)
        def _():
            for cp in x_copies(s, slot):
                cp.wait()

        @pl.when(s == 0)
        def _():
            w_copy(wg, wgv, wg_m, j, hb).wait()
            w_copy(wu, wuv, wu_m, j, hb).wait()

        cols = pl.ds(pl.multiple_of(j * hb, hb), hb)
        g = jnp.dot(xb[slot], wgv[:, cols], preferred_element_type=jnp.float32)
        u = jnp.dot(xb[slot], wuv[:, cols], preferred_element_type=jnp.float32)
        hid[:, cols] = (jax.nn.gelu(g) * u).astype(jnp.bfloat16)

        @pl.when((j == nh - 1) & (s + 2 < nc))
        def _():
            for cp in x_copies(s + 2, slot):
                cp.start()

    def down(s, i):
        q = s * npc + i

        @pl.when(s == 0)
        def _():
            w_copy(wd, wdv, wd_m, i, pw).wait()

        @pl.when(q >= SS)
        def _():
            sib_copy(q - SS).wait_send()

        cols = pl.ds(pl.multiple_of(i * pw, pw), pw)
        t = jnp.dot(hid[...], wdv[:, cols], preferred_element_type=jnp.float32)
        own[q % RO] = t[:lane]
        sst[q % SS] = t[lane:].astype(jnp.bfloat16)

        @pl.when(q >= RS)
        def _():
            pl.semaphore_wait(credit.at[q % 2], 1)

        sib_copy(q).start()

    def chip_term(q):
        return own[q % RO] + sibr[q % RS].astype(jnp.float32)

    def give_credit(q):
        @pl.when(q + RS < nq)
        def _():
            pl.semaphore_signal(credit.at[q % 2], inc=1, device_id=sib, device_id_type=MESH)

    def send_end(q):
        sib_copy(q).wait_recv()

        @pl.when(q >= LS)
        def _():
            end_copy(q - LS).wait_send()

        lst[q % LS] = chip_term(q).astype(jnp.bfloat16)
        give_credit(q)
        end_copy(q).start()

    def send_inner(q):
        k = q // 2
        sib_copy(q).wait_recv()
        end_copy(q).wait_recv()

        @pl.when(k >= LS)
        def _():
            inn_copy(q - 2 * LS).wait_send()

        lst[k % LS] = (chip_term(q) + y[at(q, c)].astype(jnp.float32)).astype(jnp.bfloat16)
        give_credit(q)
        inn_copy(q).start()

    def finish(q):
        sib_copy(q).wait_recv()
        end_copy(q).wait_recv()
        inn_copy(q).wait_recv()
        r = at(q, c)
        y[r] = (chip_term(q) + y[r].astype(jnp.float32)
                + innr[q // 2].astype(jnp.float32)).astype(jnp.bfloat16)
        give_credit(q)
        fin_inn(q).start()
        fin_out(q).start()
        fin_sib(q).start()

    def inside(q):
        return (q >= 0) & (q < nq)

    def step(it, carry):
        n = it - npc
        s, i = it // npc, it % npc

        @pl.when(mid & inside(n - LA) & ((n - LA + z) % 2 == 0))
        def _():
            send_inner(n - LA)

        @pl.when(mid & inside(n - LO) & ((n - LO + z) % 2 != 0))
        def _():
            finish(n - LO)

        @pl.when(mid & inside(n - LF) & ((n - LF + z) % 2 == 0))
        def _():
            q = n - LF
            fin_inn(q).wait_recv()
            fin_out(q).start()
            fin_sib(q).start()

        @pl.when(end & inside(n - LE))
        def _():
            q = n - LE
            fin_out(q).wait_recv()
            fin_sib(q).start()

        units = nh + npc

        def unit(k, carry):
            w = -(-(units + 1) // npc) * i + k

            @pl.when((s < nc) & (w < nh))
            def _():
                gate_up(s, w)

            @pl.when((s < nc) & (w >= nh) & (w < units))
            def _():
                down(s, w - nh)

            @pl.when(end & (s < nc) & (w > nh) & (w <= units))
            def _():
                send_end(s * npc + w - nh - 1)

            return carry

        lax.fori_loop(0, -(-(units + 1) // npc), unit, 0)
        return carry

    lax.fori_loop(0, npc + nq + max(LA, LO, LF, LE), step, 0)

    def drain(q, carry):
        sib_fin_in(q).wait_recv()
        fin_sib(q).wait_send()

        @pl.when(mid)
        def _():
            fin_out(q).wait_send()

        @pl.when(mid & ((q + z) % 2 != 0))
        def _():
            fin_inn(q).wait_send()

        @pl.when(q >= nq - SS)
        def _():
            sib_copy(q).wait_send()

        @pl.when(end & (q >= nq - LS))
        def _():
            end_copy(q).wait_send()

        @pl.when(mid & (q >= nq - 2 * LS) & ((q + z) % 2 == 0))
        def _():
            inn_copy(q).wait_send()

        return carry

    lax.fori_loop(0, nq, drain, 0)


def block(x, w_gate, w_up, w_down, lane=LANE, pw=PW, hb=HB):
    rows, d = x.shape
    ff = w_gate.shape[1]
    nq = rows // (2 * lane) * (d // pw)
    bf, f32 = jnp.bfloat16, jnp.float32
    dma = pltpu.SemaphoreType.DMA
    return pl.pallas_call(
        functools.partial(_kernel, (rows, d, ff, lane, pw, hb)),
        out_shape=pltpu.VMEM((rows, d), bf),
        in_specs=[pl.BlockSpec(memory_space=pl.ANY)] * 4,
        out_specs=pl.BlockSpec(memory_space=pltpu.VMEM),
        scratch_shapes=[
            pltpu.VMEM((d, ff), bf),
            pltpu.VMEM((d, ff), bf),
            pltpu.VMEM((ff, d), bf),
            pltpu.VMEM((2, 2 * lane, d), bf),
            pltpu.VMEM((2 * lane, ff), bf),
            pltpu.VMEM((RO, lane, pw), f32),
            pltpu.VMEM((RS, lane, pw), bf),
            pltpu.VMEM((nq // 2, lane, pw), bf),
            pltpu.VMEM((SS, lane, pw), bf),
            pltpu.VMEM((LS, lane, pw), bf),
            dma((ff // hb,)), dma((ff // hb,)), dma((d // pw,)), dma((2, 2)),
            dma((SS,)), dma((RS,)), dma((LS,)),
            dma((nq,)), dma((nq // 2,)), dma((nq,)), dma((nq,)),
            dma((nq,)), dma((nq,)), dma((nq // 2,)),
            pltpu.SemaphoreType.REGULAR((2,)),
        ],
        compiler_params=pltpu.CompilerParams(
            collective_id=0, has_side_effects=True, vmem_limit_bytes=48 * 2**20 - 64 * 1024),
    )(x, w_gate, w_up, w_down)


def solution(mesh):
    return jax.shard_map(
        block,
        mesh=mesh,
        in_specs=(P("dp", None), P(None, "tp"), P(None, "tp"), P("tp", None)),
        out_specs=P("dp", None),
        check_vma=False,
    )
```

time: 449 us -> 224 us (0.50)
  waiting for transfers between devices: 336 us -> 0 us
  Pallas kernels: 0 us -> 218 us
  matrix products: 85.9 us -> 0 us
  between operations: 13.4 us -> 0.01 us
  local copies, waits for them, and re-layouts: 14.1 us -> 6.16 us
    psum x1 -> x0, waiting for transfers between devices: 336 us -> none  [step(): return lax.psum(term, 'tp')]
    pallas_call x0 -> x1, Pallas kernels: none -> 218 us  [block(): pl.pallas_call(functools.partial(_kernel, (rows, d, ff, lane, pw, hb)), o...]
    dot_general x3 -> x0, matrix products: 85.9 us -> none  [the longest x1 29.5 us: step(): up = jnp.dot(x, w_up, preferred_element_type=jnp.float32)]
    unnamed x3 -> x1, local copies, waits for them, and re-layouts: 14.1 us -> 6.16 us
  transfers between devices with their start and end apart: 1 -> 0, of which waited for: 1 -> 0; matrix products, arithmetic and copies ran while one was open for 0% -> 0% of each run, Pallas kernels for 0% -> 0%
where the time goes in v1:
time: 224 us
  Pallas kernels  218 us (97%)
  local copies, waits for them, and re-layouts  6.16 us (3%)
    pallas_call x1, Pallas kernels, block(): pl.pallas_call(functools.partial(_kernel, (rows, d, ff, lane, pw, hb)), o...  218 us
    unnamed x1, local copies, waits for them, and re-layouts  6.16 us

profile of v1, /device:TPU:0, one launch (start us, length us, event | category | flops | bytes accessed | tf_op | source)
XLA Modules:
  0.0 223.9 jit_solution(1557371483654968548)
XLA Ops:
  0.0 217.8 %shard_map.46 = bf16[2048,4096]{1,0:T(8,128)(2,1)S(1)} custom-call(bf16[2048,4096]{1,0:T(8,128)(2,1)} %x.1, bf16[4096,1280]{1,0:T(8,128)(2,1)} %wg.1, bf16[4096,1280]{1,0:T(8,128)(2,1)} %wu.1, bf16[1280,4096]{1,0:T(8,128)(2,1)} %wd.1), custom_call_target="tpu_custom_call" | custom-call | tf_op jit(solution)/shard_map/pallas_call | solution.py:283
  217.8 6.2 %copy.6 = bf16[2048,4096]{1,0:T(8,128)(2,1)} copy(bf16[2048,4096]{1,0:T(8,128)(2,1)S(1)} %shard_map.46) | data formatting | bytes 33554432

commit v2 on v1

--- a/solution.py
+++ b/solution.py
@@ -16,7 +16,8 @@
 RO = 12
 SS = 4
 LS = 8
-LA, LO, LF, LE = 0, 2, 4, 8
+AHEAD = 2
+LA, LO, LF, LE, LD = 0, 2, 4, 8, 10
 
 
 def _kernel(cfg, x, wg, wu, wd, y, wgv, wuv, wdv, xb, hid, own, sibr, innr, sst, lst,
@@ -47,13 +48,9 @@
 
     for cp in x_copies(0, 0):
         cp.start()
-    for j in range(nh):
+    for j in range(AHEAD):
         w_copy(wg, wgv, wg_m, j, hb).start()
         w_copy(wu, wuv, wu_m, j, hb).start()
-    for j in range(npc):
-        w_copy(wd, wdv, wd_m, j, pw).start()
-    for cp in x_copies(1, 1):
-        cp.start()
 
     bar = pltpu.get_barrier_semaphore()
     pl.semaphore_signal(bar, inc=1, device_id=sib, device_id_type=MESH)
@@ -116,6 +113,21 @@
         def _():
             w_copy(wg, wgv, wg_m, j, hb).wait()
             w_copy(wu, wuv, wu_m, j, hb).wait()
+
+            @pl.when(j + AHEAD < nh)
+            def _():
+                w_copy(wg, wgv, wg_m, j + AHEAD, hb).start()
+                w_copy(wu, wuv, wu_m, j + AHEAD, hb).start()
+
+            @pl.when(j + AHEAD == nh)
+            def _():
+                for i in range(npc):
+                    w_copy(wd, wdv, wd_m, i, pw).start()
+
+        @pl.when((s == 0) & (j == nh - 1))
+        def _():
+            for cp in x_copies(1, 1):
+                cp.start()
 
         cols = pl.ds(pl.multiple_of(j * hb, hb), hb)
         g = jnp.dot(xb[slot], wgv[:, cols], preferred_element_type=jnp.float32)
@@ -193,6 +205,30 @@
         fin_out(q).start()
         fin_sib(q).start()
 
+    def drain(q):
+        sib_fin_in(q).wait_recv()
+        fin_sib(q).wait_send()
+
+        @pl.when(mid)
+        def _():
+            fin_out(q).wait_send()
+
+        @pl.when(mid & ((q + z + c) % 2 != 0))
+        def _():
+            fin_inn(q).wait_send()
+
+        @pl.when(q >= nq - SS)
+        def _():
+            sib_copy(q).wait_send()
+
+        @pl.when(end & (q >= nq - LS))
+        def _():
+            end_copy(q).wait_send()
+
+        @pl.when(mid & (q >= nq - 2 * LS) & ((q + z + c) % 2 == 0))
+        def _():
+            inn_copy(q).wait_send()
+
     def inside(q):
         return (q >= 0) & (q < nq)
 
@@ -200,15 +236,15 @@
         n = it - npc
         s, i = it // npc, it % npc
 
-        @pl.when(mid & inside(n - LA) & ((n - LA + z) % 2 == 0))
+        @pl.when(mid & inside(n - LA) & ((n - LA + z + c) % 2 == 0))
         def _():
             send_inner(n - LA)
 
-        @pl.when(mid & inside(n - LO) & ((n - LO + z) % 2 != 0))
+        @pl.when(mid & inside(n - LO) & ((n - LO + z + c) % 2 != 0))
         def _():
             finish(n - LO)
 
-        @pl.when(mid & inside(n - LF) & ((n - LF + z) % 2 == 0))
+        @pl.when(mid & inside(n - LF) & ((n - LF + z + c) % 2 == 0))
         def _():
             q = n - LF
             fin_inn(q).wait_recv()
@@ -221,10 +257,17 @@
             fin_out(q).wait_recv()
             fin_sib(q).start()
 
+        @pl.when(inside(n - LD))
+        def _():
+            drain(n - LD)
+
         units = nh + npc
+        gap = max(1, npc // (nh + 3))
+        per = -(-(npc + 1) // (npc - nh * gap))
 
         def unit(k, carry):
-            w = -(-(units + 1) // npc) * i + k
+            w = jnp.where(i < nh * gap, jnp.where((k == 0) & (i % gap == 0), i // gap, units + 1),
+                          nh + per * (i - nh * gap) + k)
 
             @pl.when((s < nc) & (w < nh))
             def _():
@@ -240,38 +283,10 @@
 
             return carry
 
-        lax.fori_loop(0, -(-(units + 1) // npc), unit, 0)
+        lax.fori_loop(0, per, unit, 0)
         return carry
 
-    lax.fori_loop(0, npc + nq + max(LA, LO, LF, LE), step, 0)
-
-    def drain(q, carry):
-        sib_fin_in(q).wait_recv()
-        fin_sib(q).wait_send()
-
-        @pl.when(mid)
-        def _():
-            fin_out(q).wait_send()
-
-        @pl.when(mid & ((q + z) % 2 != 0))
-        def _():
-            fin_inn(q).wait_send()
-
-        @pl.when(q >= nq - SS)
-        def _():
-            sib_copy(q).wait_send()
-
-        @pl.when(end & (q >= nq - LS))
-        def _():
-            end_copy(q).wait_send()
-
-        @pl.when(mid & (q >= nq - 2 * LS) & ((q + z) % 2 == 0))
-        def _():
-            inn_copy(q).wait_send()
-
-        return carry
-
-    lax.fori_loop(0, nq, drain, 0)
+    lax.fori_loop(0, npc + nq + LD, step, 0)
 
 
 def block(x, w_gate, w_up, w_down, lane=LANE, pw=PW, hb=HB):

time: 224 us -> 221 us (0.987)
  Pallas kernels: 218 us -> 214 us
    pallas_call x1, Pallas kernels: 218 us -> 214 us  [block(): pl.pallas_call(functools.partial(_kernel, (rows, d, ff, lane, pw, hb)), o...]
where the time goes in v2:
time: 221 us; the launch traced here: 220 us
  Pallas kernels  214 us (97%)
  local copies, waits for them, and re-layouts  6.16 us (3%)
    pallas_call x1, Pallas kernels, block(): pl.pallas_call(functools.partial(_kernel, (rows, d, ff, lane, pw, hb)), o...  214 us
    unnamed x1, local copies, waits for them, and re-layouts  6.16 us

profile of v2, /device:TPU:0, one launch (start us, length us, event | category | flops | bytes accessed | tf_op | source)
XLA Modules:
  0.0 220.4 jit_solution(13701554529912928383)
XLA Ops:
  0.0 214.2 %shard_map.46 = bf16[2048,4096]{1,0:T(8,128)(2,1)S(1)} custom-call(bf16[2048,4096]{1,0:T(8,128)(2,1)} %x.1, bf16[4096,1280]{1,0:T(8,128)(2,1)} %wg.1, bf16[4096,1280]{1,0:T(8,128)(2,1)} %wu.1, bf16[1280,4096]{1,0:T(8,128)(2,1)} %wd.1), custom_call_target="tpu_custom_call" | custom-call | tf_op jit(solution)/shard_map/pallas_call | solution.py:298
  214.2 6.2 %copy.6 = bf16[2048,4096]{1,0:T(8,128)(2,1)} copy(bf16[2048,4096]{1,0:T(8,128)(2,1)S(1)} %shard_map.46) | data formatting | bytes 33554432

commit v3 on v2

--- a/solution.py
+++ b/solution.py
@@ -17,6 +17,7 @@
 SS = 4
 LS = 8
 AHEAD = 2
+QS, H = 4, 2
 LA, LO, LF, LE, LD = 0, 2, 4, 8, 10
 
 
@@ -77,25 +78,47 @@
     def sib_copy(q):
         return remote(sst.at[q % SS], sibr.at[q % RS], sib_s.at[q % SS], sib_r.at[q % RS], sib)
 
-    def end_copy(q):
-        r = at(q, c)
-        return remote(lst.at[q % LS], y.at[r], lk_s.at[q % LS], out_r.at[q], inner)
-
-    def inn_copy(q):
+    def rows_of(h, n):
+        return pl.ds(h * (lane // n), lane // n)
+
+    def part(q, h, n):
+        r, cols = at(q, c)
+        return pl.ds(pl.multiple_of(r.start + h * (lane // n), lane // n), lane // n), cols
+
+    def sem(arr, base, k, h):
+        return arr.at[k if h == 0 else base + k * (H - 1) + h - 1]
+
+    def split(q, fn):
+        @pl.when(q < QS)
+        def _():
+            for h in range(H):
+                fn(h, H)
+
+        @pl.when(q >= QS)
+        def _():
+            fn(0, 1)
+
+    def end_copy(q, h, n):
+        r = part(q, h, n)
+        return remote(lst.at[q % LS, rows_of(h, n)], y.at[r], sem(lk_s, LS, q % LS, h),
+                      sem(out_r, nq, q, h), inner)
+
+    def inn_copy(q, h, n):
         k = q // 2
-        return remote(lst.at[k % LS], innr.at[k], lk_s.at[k % LS], inn_r.at[k], inner)
+        return remote(lst.at[k % LS, rows_of(h, n)], innr.at[k, rows_of(h, n)],
+                      sem(lk_s, LS, k % LS, h), sem(inn_r, nq // 2, k, h), inner)
 
     def fin_sib(q):
         r = at(q, c)
         return remote(y.at[r], y.at[r], fs_sib.at[q], sf_r.at[q], sib)
 
-    def fin_out(q):
-        r = at(q, c)
-        return remote(y.at[r], y.at[r], fs_out.at[q], fin_r.at[q], outer)
-
-    def fin_inn(q):
-        r = at(q, c)
-        return remote(y.at[r], y.at[r], fs_inn.at[q // 2], fin_r.at[q], inner)
+    def fin_out(q, h, n):
+        r = part(q, h, n)
+        return remote(y.at[r], y.at[r], sem(fs_out, nq, q, h), sem(fin_r, nq, q, h), outer)
+
+    def fin_inn(q, h, n):
+        r = part(q, h, n)
+        return remote(y.at[r], y.at[r], sem(fs_inn, nq // 2, q // 2, h), sem(fin_r, nq, q, h), inner)
 
     def sib_fin_in(q):
         r = at(q, 1 - c)
@@ -161,8 +184,8 @@
 
         sib_copy(q).start()
 
-    def chip_term(q):
-        return own[q % RO] + sibr[q % RS].astype(jnp.float32)
+    def chip_term(q, h, n):
+        return own[q % RO, rows_of(h, n)] + sibr[q % RS, rows_of(h, n)].astype(jnp.float32)
 
     def give_credit(q):
         @pl.when(q + RS < nq)
@@ -174,35 +197,54 @@
 
         @pl.when(q >= LS)
         def _():
-            end_copy(q - LS).wait_send()
-
-        lst[q % LS] = chip_term(q).astype(jnp.bfloat16)
+            split(q - LS, lambda h, n: end_copy(q - LS, h, n).wait_send())
+
+        def go(h, n):
+            lst[q % LS, rows_of(h, n)] = chip_term(q, h, n).astype(jnp.bfloat16)
+            end_copy(q, h, n).start()
+
+        split(q, go)
         give_credit(q)
-        end_copy(q).start()
 
     def send_inner(q):
         k = q // 2
         sib_copy(q).wait_recv()
-        end_copy(q).wait_recv()
 
         @pl.when(k >= LS)
         def _():
-            inn_copy(q - 2 * LS).wait_send()
-
-        lst[k % LS] = (chip_term(q) + y[at(q, c)].astype(jnp.float32)).astype(jnp.bfloat16)
+            split(q - 2 * LS, lambda h, n: inn_copy(q - 2 * LS, h, n).wait_send())
+
+        def go(h, n):
+            end_copy(q, h, n).wait_recv()
+            lst[k % LS, rows_of(h, n)] = (
+                chip_term(q, h, n) + y[part(q, h, n)].astype(jnp.float32)).astype(jnp.bfloat16)
+            inn_copy(q, h, n).start()
+
+        split(q, go)
         give_credit(q)
-        inn_copy(q).start()
 
     def finish(q):
         sib_copy(q).wait_recv()
-        end_copy(q).wait_recv()
-        inn_copy(q).wait_recv()
-        r = at(q, c)
-        y[r] = (chip_term(q) + y[r].astype(jnp.float32)
-                + innr[q // 2].astype(jnp.float32)).astype(jnp.bfloat16)
+
+        def go(h, n):
+            end_copy(q, h, n).wait_recv()
+            inn_copy(q, h, n).wait_recv()
+            r = part(q, h, n)
+            y[r] = (chip_term(q, h, n) + y[r].astype(jnp.float32)
+                    + innr[q // 2, rows_of(h, n)].astype(jnp.float32)).astype(jnp.bfloat16)
+            fin_inn(q, h, n).start()
+            fin_out(q, h, n).start()
+
+        split(q, go)
         give_credit(q)
-        fin_inn(q).start()
-        fin_out(q).start()
+        fin_sib(q).start()
+
+    def forward(q):
+        def go(h, n):
+            fin_inn(q, h, n).wait_recv()
+            fin_out(q, h, n).start()
+
+        split(q, go)
         fin_sib(q).start()
 
     def drain(q):
@@ -211,11 +253,11 @@
 
         @pl.when(mid)
         def _():
-            fin_out(q).wait_send()
+            split(q, lambda h, n: fin_out(q, h, n).wait_send())
 
         @pl.when(mid & ((q + z + c) % 2 != 0))
         def _():
-            fin_inn(q).wait_send()
+            split(q, lambda h, n: fin_inn(q, h, n).wait_send())
 
         @pl.when(q >= nq - SS)
         def _():
@@ -223,11 +265,11 @@
 
         @pl.when(end & (q >= nq - LS))
         def _():
-            end_copy(q).wait_send()
+            end_copy(q, 0, 1).wait_send()
 
         @pl.when(mid & (q >= nq - 2 * LS) & ((q + z + c) % 2 == 0))
         def _():
-            inn_copy(q).wait_send()
+            inn_copy(q, 0, 1).wait_send()
 
     def inside(q):
         return (q >= 0) & (q < nq)
@@ -246,15 +288,12 @@
 
         @pl.when(mid & inside(n - LF) & ((n - LF + z + c) % 2 == 0))
         def _():
-            q = n - LF
-            fin_inn(q).wait_recv()
-            fin_out(q).start()
-            fin_sib(q).start()
+            forward(n - LF)
 
         @pl.when(end & inside(n - LE))
         def _():
             q = n - LE
-            fin_out(q).wait_recv()
+            split(q, lambda h, n: fin_out(q, h, n).wait_recv())
             fin_sib(q).start()
 
         @pl.when(inside(n - LD))
@@ -294,6 +333,7 @@
     ff = w_gate.shape[1]
     nq = rows // (2 * lane) * (d // pw)
     bf, f32 = jnp.bfloat16, jnp.float32
+    more = QS * (H - 1)
     dma = pltpu.SemaphoreType.DMA
     return pl.pallas_call(
         functools.partial(_kernel, (rows, d, ff, lane, pw, hb)),
@@ -312,9 +352,9 @@
             pltpu.VMEM((SS, lane, pw), bf),
             pltpu.VMEM((LS, lane, pw), bf),
             dma((ff // hb,)), dma((ff // hb,)), dma((d // pw,)), dma((2, 2)),
-            dma((SS,)), dma((RS,)), dma((LS,)),
-            dma((nq,)), dma((nq // 2,)), dma((nq,)), dma((nq,)),
-            dma((nq,)), dma((nq,)), dma((nq // 2,)),
+            dma((SS,)), dma((RS,)), dma((LS * H,)),
+            dma((nq + more,)), dma((nq // 2 + more,)), dma((nq + more,)), dma((nq,)),
+            dma((nq,)), dma((nq + more,)), dma((nq // 2 + more,)),
             pltpu.SemaphoreType.REGULAR((2,)),
         ],
         compiler_params=pltpu.CompilerParams(

time: 221 us -> 221 us (level)
  no operation moved by 1% of the time
where the time goes in v3:
time: 221 us
  Pallas kernels  214 us (97%)
  local copies, waits for them, and re-layouts  6.16 us (3%)
    pallas_call x1, Pallas kernels, block(): pl.pallas_call(functools.partial(_kernel, (rows, d, ff, lane, pw, hb)), o...  214 us
    unnamed x1, local copies, waits for them, and re-layouts  6.16 us

profile of v3, /device:TPU:0, one launch (start us, length us, event | category | flops | bytes accessed | tf_op | source)
XLA Modules:
  0.0 220.5 jit_solution(6119194814266363914)
XLA Ops:
  0.0 214.4 %shard_map.46 = bf16[2048,4096]{1,0:T(8,128)(2,1)S(1)} custom-call(bf16[2048,4096]{1,0:T(8,128)(2,1)} %x.1, bf16[4096,1280]{1,0:T(8,128)(2,1)} %wg.1, bf16[4096,1280]{1,0:T(8,128)(2,1)} %wu.1, bf16[1280,4096]{1,0:T(8,128)(2,1)} %wd.1), custom_call_target="tpu_custom_call" | custom-call | tf_op jit(solution)/shard_map/pallas_call | solution.py:338
  214.4 6.2 %copy.6 = bf16[2048,4096]{1,0:T(8,128)(2,1)} copy(bf16[2048,4096]{1,0:T(8,128)(2,1)S(1)} %shard_map.46) | data formatting | bytes 33554432
